TPU v7x, 32 devices: a whole 2x2x4 slice. The times are simulated.
32 devices in a mesh: groups: 2 (over x), lat: 16 (over z, y, core).
Axes of the slice: x: 2, y: 2, z: 4, core: 2. Of those that a mesh axis runs over, the one named last changes fastest.
Arguments:
- inputs: bfloat16 [1024, 4608], P('groups', 'lat'), parts along dimension 0, may hold values from -6 to 6
- w_enc: bfloat16 [9216, 8192], P('groups', 'lat'), parts along dimension 0, may hold values from -0.09375 to 0.09375
- b_enc: float32 [16384], P(('groups', 'lat')), parts along dimension 0, may hold values from -3 to 3
- thresholds: float32 [16384], P(('groups', 'lat')), parts along dimension 0, may hold values from 0.1 to 4
- w_dec: bfloat16 [16384, 4608], P(('groups', 'lat')), parts along dimension 0, may hold values from -0.1875 to 0.1875
- b_dec: bfloat16 [9216], P(('groups', 'lat')), parts along dimension 0, may hold values from -5 to 5
- sparsity: float32 [2], P('groups'), parts along dimension 0, may hold values from 1 to 4
Outputs:
- grad_enc: bfloat16 [9216, 8192], P('groups', 'lat'), parts along dimension 0
- grad_b_enc: float32 [16384], P(('groups', 'lat')), parts along dimension 0
- grad_dec: bfloat16 [16384, 4608], P(('groups', 'lat')), parts along dimension 0
- grad_b_dec: float32 [9216], P(('groups', 'lat')), parts along dimension 0
- loss_terms: float32 [4], P('groups'), parts along dimension 0
There are 2 independent parts, one for each index of `groups`. A program takes and returns all parts, laid end to end along the dimension named above; each array names one. Nothing has to cross between parts.
All inputs are finite; a program needn't handle non-finite values.
Results may differ from a plain program's by a relative error of at most 0.006.
Values may be sent and summed in bfloat16 or wider, within the bound.
A program may use at most 128 MiB of HBM per device.

v0:
```python
import jax
import jax.numpy as jnp
from jax import lax
from jax.sharding import PartitionSpec as P


def on_device(inputs, w_enc, b_enc, thresholds, w_dec, b_dec, sparsity):
    cols = inputs.shape[1]
    parts = lax.axis_size("lat")
    joined, dec_bias = (
        lax.all_gather(inputs, "lat", axis=1, tiled=True),
        lax.all_gather(b_dec.reshape(1, cols), "lat", axis=1, tiled=True),
    )
    rows = joined.shape[0]
    width = joined.shape[1]
    latent_local = w_enc.shape[1]
    pre = jnp.dot(joined, w_enc, preferred_element_type=jnp.float32) + b_enc
    gate = jax.nn.sigmoid((pre - thresholds) / 0.05)
    feats = (pre * gate).astype(jnp.bfloat16)
    partial_value = jnp.dot(feats, w_dec, preferred_element_type=jnp.float32)
    count = jnp.sum(gate)
    recon = lax.psum_scatter(partial_value, "lat", scatter_dimension=1, tiled=True) + b_dec.astype(
        jnp.float32
    )
    err = recon - inputs.astype(jnp.float32)
    scaled = 2.0 / rows * err
    grad_b_dec = jnp.sum(scaled, axis=0)
    sq_sum, count_all = lax.psum((jnp.sum(err * err), count), "lat")
    error_bf = lax.all_gather(scaled.astype(jnp.bfloat16), "lat", axis=1, tiled=True)
    grad_dec = lax.dot_general(
        feats, error_bf, (((0,), (0,)), ((), ())), preferred_element_type=jnp.float32
    ).astype(jnp.bfloat16)
    g_feats = lax.dot_general(
        error_bf, w_dec, (((1,), (1,)), ((), ())), preferred_element_type=jnp.float32
    )
    g_pre = g_feats * (gate + pre * gate * (1.0 - gate) / 0.05)
    g_pre_bf = g_pre.astype(jnp.bfloat16)
    grad_b_enc = jnp.sum(g_pre, axis=0)
    grad_enc = lax.dot_general(
        joined, g_pre_bf, (((0,), (0,)), ((), ())), preferred_element_type=jnp.float32
    ).astype(jnp.bfloat16)
    loss_terms = jnp.stack(
        [sq_sum / (rows * width), sparsity[0] * count_all / (rows * latent_local * parts)]
    )
    return (grad_enc, grad_b_enc, grad_dec, grad_b_dec, loss_terms)


def solution(mesh):
    return jax.shard_map(
        on_device,
        mesh=mesh,
        in_specs=(
            P("groups", "lat"),
            P("groups", "lat"),
            P(("groups", "lat")),
            P(("groups", "lat")),
            P(("groups", "lat"), None),
            P(("groups", "lat")),
            P("groups"),
        ),
        out_specs=(
            P("groups", "lat"),
            P(("groups", "lat")),
            P(("groups", "lat"), None),
            P(("groups", "lat")),
            P("groups"),
        ),
        check_vma=False,
    )
```

profile of v0, /device:TPU:1, one launch (start us, length us, event | category | flops | bytes accessed | tf_op | source)
XLA Modules:
  0.0 281.4 jit_solution(2307276209786668930)
XLA Ops:
  7.2 0.0 all-gather.3.cloned.1.call-start
  7.2 0.7 all-gather.3.cloned.1.call-update
  7.9 0.0 copy-start.2
  7.9 0.0 reduce-scatter.2.cloned.1.call-start
  8.0 57.9 %all-gather.3.cloned.1.call-done = bf16[512,4608]{0,1:T(8,128)(2,1)} async-done(((bf16[512,288]{0,1:T(8,128)(2,1)}), bf16[512,4608]{0,1:T(8,128)(2,1)}) %all-gather.3.cloned.1.call-update) | async-done | bytes 4718608 | tf_op jit(solution)/shard_map/all_gather | solution.py:11
  65.9 7.4 %fusion.2 = (f32[]{:T(128)}, f32[512,512]{1,0:T(8,128)S(1)}) fusion(f32[512]{0:T(512)} %param.10, f32[512]{0:T(512)} %param.9, bf16[512,4608]{0,1:T(8,128)(2,1)} %all-gather.3.cloned.1.call-done, bf16[4608,512]{1,0:T(8,128)(2,1)} %param.8), kind=kOutput, calls=%fused_computation.13 | convolution fusion | flops 2417754112 | bytes 10489860 | tf_op jit(solution)/shard_map/dot_general | solution.py:17
  73.3 0.0 copy-done.2
  73.3 8.6 %fusion.3 = f32[512,4608]{0,1:T(8,128)} fusion(bf16[512,4608]{1,0:T(8,128)(2,1)} %param.11, f32[512,512]{1,0:T(8,128)S(1)} %get-tuple-element.18, f32[512]{0:T(512)S(1)} %copy-done.2), kind=kOutput, calls=%fused_computation.14 | convolution fusion | flops 2417754112 | bytes 15206400 | tf_op jit(solution)/shard_map/dot_general | solution.py:20
  81.9 0.0 copy-start.1
  81.9 0.0 copy-start
  81.9 0.0 reduce-scatter.2.cloned.1.call-update
  81.9 0.0 all-gather.5.cloned.1.call-start
  82.0 0.6 copy-done.1
  82.6 108.6 %reduce-scatter.2.cloned.1.call-done = f32[512,288]{0,1:T(8,128)} async-done(((f32[512,4608]{0,1:T(8,128)}), f32[512,288]{0,1:T(8,128)}) %reduce-scatter.2.cloned.1.call-update) | async-done | bytes 589840 | tf_op jit(solution)/shard_map/reduce_scatter | solution.py:22
  191.2 0.0 copy-done
  191.2 2.7 multiply_reduce_fusion
  193.8 0.0 all-gather.5.cloned.1.call-update
  194.5 30.6 %all-reduce = (f32[]{:T(128)}, f32[]{:T(128)}) all-reduce(f32[]{:T(128)} %get-tuple-element.17, f32[]{:T(128)} %get-tuple-element.10), channel_id=1, replica_groups=mesh['groups'=2,'lat'=16] {'lat'}, use_global_device_ids=true, to_apply=%region_6.0 | all-reduce | flops 2 | bytes 16 | tf_op jit(solution)/shard_map/psum | solution.py:28
  226.4 0.6 pad_maximum_fusion
  227.0 20.6 %all-gather.5.cloned.1.call-done = bf16[512,4608]{0,1:T(8,128)(2,1)} async-done(((bf16[512,288]{0,1:T(8,128)(2,1)}), bf16[512,4608]{0,1:T(8,128)(2,1)}) %all-gather.5.cloned.1.call-update) | async-done | bytes 4718608 | tf_op jit(solution)/shard_map/all_gather | solution.py:29
  247.6 7.3 %fusion.4 = (f32[512]{0:T(512)}, bf16[512,512]{1,0:T(8,128)(2,1)S(1)}) fusion(f32[512,512]{1,0:T(8,128)S(1)} %get-tuple-element.18, f32[512]{0:T(512)S(1)} %copy-done.2, bf16[512,4608]{0,1:T(8,128)(2,1)} %all-gather.5.cloned.1.call-done, bf16[512,4608]{1,0:T(8,128)(2,1)} %param.11), kind=kOutput, calls=%fused_computation.15 | convolution fusion | flops 2419326464 | bytes 11014144 | tf_op jit(solution)/shard_map/dot_general | solution.py:33
  254.9 6.7 %fusion = bf16[4608,512]{0,1:T(8,128)(2,1)} fusion(bf16[512,4608]{0,1:T(8,128)(2,1)} %all-gather.3.cloned.1.call-done, bf16[512,512]{1,0:T(8,128)(2,1)S(1)} %get-tuple-element.16), kind=kOutput, calls=%fused_computation.2 | convolution fusion | flops 2418278400 | bytes 9961472 | tf_op jit(solution)/shard_map/dot_general | solution.py:39
  261.5 6.6 %copy.12 = bf16[4608,512]{1,0:T(8,128)(2,1)} copy(bf16[4608,512]{0,1:T(8,128)(2,1)} %fusion) | data formatting | bytes 9437184
  268.2 6.7 %convolution_convert_fusion = bf16[512,4608]{1,0:T(8,128)(2,1)} fusion(bf16[512,4608]{0,1:T(8,128)(2,1)} %all-gather.5.cloned.1.call-done, f32[512,512]{1,0:T(8,128)S(1)} %get-tuple-element.18, f32[512]{0:T(512)S(1)} %copy-done.2), kind=kOutput, calls=%fused_computation | convolution fusion | flops 2420113408 | bytes 10487808 | tf_op jit(solution)/shard_map/dot_general | solution.py:30
  (1 shorter events, 0.0 us)
Async XLA Ops:
  7.2 58.7 %all-gather.3.cloned.1.call-start = ((), (), s32[]{:S(2)}) async-start(), calls=%async_computation.1 | async-start | bytes 5013504 | tf_op jit(solution)/shard_map/all_gather | solution.py:11
  7.9 65.4 %copy-start.2 = (f32[512]{0:T(512)S(1)}, f32[512]{0:T(512)}, u32[]{:S(2)}) copy-start(f32[512]{0:T(512)} %param.10) | copy-start | bytes 6148
  7.9 183.2 %reduce-scatter.2.cloned.1.call-start = ((), (), s32[]{:S(2)}) async-start(), calls=%async_computation.2 | async-start | bytes 10027008 | tf_op jit(solution)/shard_map/reduce_scatter | solution.py:22
  81.9 0.7 copy-start.1
  81.9 109.3 %copy-start = (bf16[512,288]{0,1:T(8,128)(2,1)S(1)}, bf16[512,288]{0,1:T(8,128)(2,1)}, u32[]{:S(2)}) copy-start(bf16[512,288]{0,1:T(8,128)(2,1)} %param.7) | copy-start | bytes 884740
  81.9 165.7 %all-gather.5.cloned.1.call-start = ((), (), s32[]{:S(2)}) async-start(), calls=%async_computation.3 | async-start | bytes 5013504 | tf_op jit(solution)/shard_map/all_gather | solution.py:29
Sparse Core Ops, SparseCore 0:
  10.3 55.5 all-gather.2
  82.0 109.0 reduce-scatter.1
  194.0 53.5 all-gather.4
where the time goes:
time: 282 us; the launch traced here: 281 us
  waiting for transfers between devices  188 us (67%)
  matrix products  36.7 us (13%)
  blocking collectives  30.6 us (11%)
  between operations  15.7 us (6%)
  local copies, waits for them, and re-layouts  7.23 us (3%)
  other arithmetic  3.24 us (1%)
    reduce_scatter x1, waiting for transfers between devices, on_device(): lax.psum_scatter(partial_value, 'lat', scatter_dimension=1, tiled=True)  109 us
    all_gather x1, waiting for transfers between devices, on_device(): lax.all_gather(inputs, 'lat', axis=1, tiled=True)  57.9 us
    psum x1, blocking collectives, on_device(): sq_sum, count_all = lax.psum((jnp.sum(err * err), count), 'lat')  30.6 us
    all_gather x1, waiting for transfers between devices, on_device(): lax.all_gather(scaled.astype(jnp.bfloat16), 'lat', axis=1, tiled=True)  20.6 us
    dot_general x1, matrix products, on_device(): partial_value = jnp.dot(feats, w_dec, preferred_element_type=jnp.float32)  8.59 us
    dot_general x1, matrix products, on_device(): pre = jnp.dot(joined, w_enc, preferred_element_type=jnp.float32) + b_enc  7.39 us
    dot_general x1, matrix products, on_device(): lax.dot_general(error_bf, w_dec, (((1,), (1,)), ((), ())), preferred_elem...  7.28 us
    unnamed x7, local copies, waits for them, and re-layouts  7.23 us
  transfers between devices with their start and end apart: 3, of which 3 were waited for; matrix products, arithmetic and copies ran while one was open for 0% of the time, Pallas kernels for 0%

commit v1 on v0

v1 whole, which is shorter than its diff:
```python
import functools

import jax
import jax.numpy as jnp
from jax import lax
from jax.experimental import pallas as pl
from jax.experimental.pallas import tpu as pltpu
from jax.sharding import PartitionSpec as P

MESH = pl.DeviceIdType.MESH
F32 = jnp.float32
BF16 = jnp.bfloat16


def dot(a, b, ca, cb):
    return lax.dot_general(a, b, (((ca,), (cb,)), ((), ())), preferred_element_type=F32)


def step_kernel(
    n, inner, rows_total,
    x_ref, wenc_hbm, wdec_hbm, benc_ref, thr_ref, bdec_ref,
    xt_hbm, et_hbm, ft_ref, gp_ref, gbenc_ref, gbdec_ref, stats_ref,
    xt, et, wenc, wdec, wdt, pre, dg, theirs, given, mine, sbuf, rbuf, st,
    load_sem, out_sem,
    a_ss, a_rs, a_ds, a_dr, r_ss, r_rs, r_ds, r_dr, e_ss, e_rs, e_ds, e_dr,
):
    blk, half = x_ref.shape[1], x_ref.shape[2]
    depth, lat = wenc.shape
    subs = 2 if blk % 32 == 0 else 1
    sub_rows = blk // subs
    me = lax.axis_index("lat")
    core = lax.rem(me, 2)
    chip = me // 2
    m = n // 2

    if inner == 2:
        y0 = lax.rem(chip, 2)
        z0 = chip // 2
        pos = z0 + y0 * (2 * m - 1 - 2 * z0)
    else:
        pos = chip

    def chip_at(p):
        p = lax.rem(p + 2 * n, n)
        if inner == 2:
            y = p // m
            z = p + y * (2 * m - 1 - 2 * p)
            return 2 * z + y
        return p

    nxt = 2 * chip_at(pos + 1) + core
    prv = 2 * chip_at(pos - 1) + core
    mate = me + 1 - 2 * core

    barrier = pltpu.get_barrier_semaphore()
    for peer in (nxt, prv, mate):
        pl.semaphore_signal(barrier, inc=1, device_id={"lat": peer}, device_id_type=MESH)

    own_rows = pl.ds(pl.multiple_of(me * blk, 16), blk)
    load_enc = pltpu.make_async_copy(wenc_hbm, wenc, load_sem.at[0])
    load_dec = pltpu.make_async_copy(wdec_hbm, wdec, load_sem.at[1])
    load_x = pltpu.make_async_copy(x_ref, xt.at[:, own_rows], load_sem.at[2])
    load_x.start()
    load_enc.start()
    load_dec.start()
    load_x.wait()
    pl.semaphore_wait(barrier, 3)

    def remote(src, dst, ss, rs, peer):
        return pltpu.make_async_remote_copy(
            src_ref=src, dst_ref=dst, send_sem=ss, recv_sem=rs,
            device_id={"lat": peer}, device_id_type=MESH,
        )

    def make_gather(buf, with_stats, ss, rs, ds, dr):
        flows = [(h, u) for h in range(2) for u in range(subs)]
        if with_stats:
            flows.append((0, -1))

        def piece(f, dev):
            h, u = flows[f]
            if u < 0:
                return st.at[dev]
            return buf.at[h, pl.ds(pl.multiple_of(dev * blk + u * sub_rows, 16), sub_rows)]

        def dev_at(f, s, c):
            sign = 1 if flows[f][0] == 0 else -1
            return 2 * chip_at(pos - sign * s) + c

        def ring(f, s):
            r = piece(f, dev_at(f, s, core))
            return remote(r, r, ss.at[f, s], rs.at[f, s], nxt if flows[f][0] == 0 else prv)

        def ring_in(f, s):
            r = piece(f, dev_at(f, s + 1, core))
            return remote(r, r, ss.at[f, s], rs.at[f, s], nxt if flows[f][0] == 0 else prv)

        def d2d(f, s):
            r = piece(f, dev_at(f, s, core))
            return remote(r, r, ds.at[f, s], dr.at[f, s], mate)

        def d2d_in(f, s):
            r = piece(f, dev_at(f, s, 1 - core))
            return remote(r, r, ds.at[f, s], dr.at[f, s], mate)

        count = range(len(flows))

        def run(first, compute):
            for f in count:
                ring(f, 0).start()
            for f in count:
                d2d(f, 0).start()
            first()

            def arrive(s):
                for f in count:
                    d2d_in(f, s).wait_recv()

            @pl.loop(1, n - 1)
            def _(s):
                for f in count:
                    ring_in(f, s - 1).wait_recv()
                    ring(f, s).start()
                    d2d(f, s).start()
                arrive(s - 1)
                compute(s - 1)

            for f in count:
                ring_in(f, n - 2).wait_recv()
                d2d(f, n - 1).start()
            arrive(n - 2)
            compute(n - 2)
            arrive(n - 1)
            compute(n - 1)

            @pl.loop(0, n - 1)
            def _(s):
                for f in count:
                    ring(f, s).wait_send()

            @pl.loop(0, n)
            def _(s):
                for f in count:
                    d2d(f, s).wait_send()

        return run

    def first():
        pre[...] = jnp.zeros_like(pre)
        load_dec.wait()

        @pl.loop(0, depth // 128)
        def _(i):
            c = pl.ds(pl.multiple_of(i * 128, 128), 128)
            wdt[c, :] = wdec[:, c].T

        load_enc.wait()

    def encode(s):
        for h in range(2):
            q = chip_at(pos - s if h == 0 else pos + s)
            r = pl.ds(pl.multiple_of(q * 2 * blk, 16), 2 * blk)
            pre[h] += dot(wenc[r, :], xt[h, r, :], 0, 0)

    make_gather(xt, False, a_ss, a_rs, a_ds, a_dr)(first, encode)
    out_x = pltpu.make_async_copy(xt, xt_hbm, out_sem.at[0])
    out_x.start()

    total = jnp.zeros((1, half), F32)
    for h in range(2):
        p = pre[h] + benc_ref[...]
        gate = jax.nn.sigmoid((p - thr_ref[...]) / 0.05)
        ft_ref[h] = (p * gate).astype(BF16)
        dg[h] = gate + p * gate * (1.0 - gate) / 0.05
        total = total + jnp.sum(gate, axis=0, keepdims=True)

    def block_at(h, t):
        return chip_at(pos - 1 - t if h == 0 else pos + 1 + t)

    def swap(h, t):
        return remote(theirs.at[h, t], given.at[h, t], r_ds.at[h, t], r_dr.at[h, t], mate)

    def partial(t):
        for h in range(2):
            q = block_at(h, t)
            other = pl.ds(pl.multiple_of((2 * q + 1 - core) * blk, 16), blk)
            theirs[h, t] = dot(wdt[other, :], ft_ref[h], 1, 0).astype(BF16)
            swap(h, t).start()
        for h in range(2):
            q = block_at(h, t)
            same = pl.ds(pl.multiple_of((2 * q + core) * blk, 16), blk)
            mine[h, t] = dot(wdt[same, :], ft_ref[h], 1, 0)

    def pass_on(h, u, s):
        r = pl.ds(u * sub_rows, sub_rows)
        f = h * subs + u
        return remote(
            sbuf.at[h, s, r], rbuf.at[h, s, r], r_ss.at[f, s], r_rs.at[f, s], nxt if h == 0 else prv
        )

    def hop(s, has_input):
        for h in range(2):
            swap(h, s).wait_recv()
        for u in range(subs):
            for h in range(2):
                r = pl.ds(u * sub_rows, sub_rows)
                v = mine[h, s, r, :] + given[h, s, r, :].astype(F32)
                if has_input:
                    pass_on(h, u, s - 1).wait_recv()
                    v = v + rbuf[h, s - 1, r, :].astype(F32)
                sbuf[h, s, r, :] = v.astype(BF16)
                pass_on(h, u, s).start()

    partial(0)
    partial(1)
    hop(0, False)
    partial(2)

    @pl.loop(1, n - 2)
    def _(s):
        hop(s, True)
        partial(s + 2)

    hop(n - 2, True)
    sq = jnp.zeros((1, half), F32)
    gb = jnp.zeros((blk, 1), F32)
    for h in range(2):
        swap(h, n - 1).wait_recv()
        for u in range(subs):
            pass_on(h, u, n - 2).wait_recv()
        recon = mine[h, n - 1] + given[h, n - 1].astype(F32) + rbuf[h, n - 2].astype(F32) + bdec_ref[...]
        err = recon - x_ref[h].astype(F32)
        scaled = (2.0 / rows_total) * err
        et[h, own_rows, :] = scaled.astype(BF16)
        sq = sq + jnp.sum(err * err, axis=0, keepdims=True)
        gb = gb + jnp.sum(scaled, axis=1, keepdims=True)
    gbdec_ref[...] = gb
    lane = lax.broadcasted_iota(jnp.int32, (8, 128), 0)
    st[me] = jnp.where(lane == 0, jnp.sum(sq), jnp.sum(total))

    def nothing(*_):
        pass

    make_gather(et, True, e_ss, e_rs, e_ds, e_dr)(nothing, nothing)
    out_e = pltpu.make_async_copy(et, et_hbm, out_sem.at[1])
    out_e.start()

    @pl.loop(0, n - 1)
    def _(s):
        for h in range(2):
            for u in range(subs):
                pass_on(h, u, s).wait_send()

    @pl.loop(0, n)
    def _(s):
        for h in range(2):
            swap(h, s).wait_send()

    chunk = next(c for c in range(1152, 0, -128) if depth % c == 0)
    gsum = jnp.zeros((lat, 1), F32)
    for h in range(2):
        pre[h] = jnp.zeros_like(pre[h])

        @pl.loop(0, depth // chunk)
        def _(i):
            c = pl.ds(pl.multiple_of(i * chunk, 128), chunk)
            pre[h] += dot(wdec[:, c], et[h, c, :], 1, 0)

        g = pre[h] * dg[h]
        gp_ref[h] = g.astype(BF16)
        gsum = gsum + jnp.sum(g, axis=1, keepdims=True)
    gbenc_ref[...] = gsum
    stats_ref[...] = jnp.sum(st[...], axis=0)
    out_x.wait()
    out_e.wait()


def grads_kernel(xt_ref, et_ref, ft_ref, gp_ref, genc_ref, gdec_ref):
    genc_ref[...] = (dot(xt_ref[0], gp_ref[0], 1, 1) + dot(xt_ref[1], gp_ref[1], 1, 1)).astype(BF16)
    gdec_ref[...] = (dot(ft_ref[0], et_ref[0], 1, 1) + dot(ft_ref[1], et_ref[1], 1, 1)).astype(BF16)


def on_device(inner, inputs, w_enc, b_enc, thresholds, w_dec, b_dec, sparsity):
    rows, blk = inputs.shape
    parts = lax.axis_size("lat")
    n = parts // 2
    depth, lat = w_enc.shape
    half = rows // 2
    subs = 2 if blk % 32 == 0 else 1
    nf = 2 * subs
    x_blocks = jnp.transpose(inputs.reshape(2, half, blk), (0, 2, 1))
    vmem = pl.BlockSpec(memory_space=pltpu.VMEM)
    hbm = pl.BlockSpec(memory_space=pl.ANY)
    dma = pltpu.SemaphoreType.DMA
    xt, et, ft, gp, gbenc, gbdec, stats = pl.pallas_call(
        functools.partial(step_kernel, n, inner, rows),
        out_shape=(
            jax.ShapeDtypeStruct((2, depth, half), BF16),
            jax.ShapeDtypeStruct((2, depth, half), BF16),
            jax.ShapeDtypeStruct((2, lat, half), BF16),
            jax.ShapeDtypeStruct((2, lat, half), BF16),
            jax.ShapeDtypeStruct((lat, 1), F32),
            jax.ShapeDtypeStruct((blk, 1), F32),
            jax.ShapeDtypeStruct((8, 128), F32),
        ),
        in_specs=[vmem, hbm, hbm, vmem, vmem, vmem],
        out_specs=(hbm, hbm, vmem, vmem, vmem, vmem, vmem),
        scratch_shapes=[
            pltpu.VMEM((2, depth, half), BF16),
            pltpu.VMEM((2, depth, half), BF16),
            pltpu.VMEM((depth, lat), BF16),
            pltpu.VMEM((lat, depth), BF16),
            pltpu.VMEM((depth, lat), BF16),
            pltpu.VMEM((2, lat, half), F32),
            pltpu.VMEM((2, lat, half), F32),
            pltpu.VMEM((2, n, blk, half), BF16),
            pltpu.VMEM((2, n, blk, half), BF16),
            pltpu.VMEM((2, n, blk, half), F32),
            pltpu.VMEM((2, n - 1, blk, half), BF16),
            pltpu.VMEM((2, n - 1, blk, half), BF16),
            pltpu.VMEM((parts, 8, 128), F32),
            dma((3,)),
            dma((2,)),
            dma((nf, n - 1)), dma((nf, n - 1)), dma((nf, n)), dma((nf, n)),
            dma((nf, n - 1)), dma((nf, n - 1)), dma((2, n)), dma((2, n)),
            dma((nf + 1, n - 1)), dma((nf + 1, n - 1)), dma((nf + 1, n)), dma((nf + 1, n)),
        ],
        compiler_params=pltpu.CompilerParams(
            collective_id=0, has_side_effects=True, vmem_limit_bytes=63 * 1024 * 1024
        ),
        name="sae_step",
    )(
        x_blocks, w_enc, w_dec, b_enc.reshape(lat, 1), thresholds.reshape(lat, 1),
        b_dec.astype(F32).reshape(blk, 1),
    )
    tile = 512 if depth % 512 == 0 else 128
    grad_enc, grad_dec = pl.pallas_call(
        grads_kernel,
        grid=(depth // tile,),
        out_shape=(
            jax.ShapeDtypeStruct((depth, lat), BF16),
            jax.ShapeDtypeStruct((lat, depth), BF16),
        ),
        in_specs=[
            pl.BlockSpec((2, tile, half), lambda i: (0, i, 0)),
            pl.BlockSpec((2, tile, half), lambda i: (0, i, 0)),
            pl.BlockSpec((2, lat, half), lambda i: (0, 0, 0)),
            pl.BlockSpec((2, lat, half), lambda i: (0, 0, 0)),
        ],
        out_specs=(
            pl.BlockSpec((tile, lat), lambda i: (i, 0)),
            pl.BlockSpec((lat, tile), lambda i: (0, i)),
        ),
        name="sae_grads",
    )(xt, et, ft, gp)
    loss_terms = jnp.stack(
        [
            stats[0, 0] / (rows * depth),
            sparsity[0] * stats[1, 0] / (rows * lat * parts),
        ]
    )
    return grad_enc, gbenc.reshape(lat), grad_dec, gbdec.reshape(blk), loss_terms


def chips_inner(mesh):
    try:
        where = [tuple(d.coords) for d in mesh.devices.reshape(-1, mesh.shape["lat"])[0][::2]]
    except AttributeError:
        return 1
    if len(where) < 4 or len(where) % 2:
        return 1
    moved = [sum(a != b for a, b in zip(where[0], w)) for w in (where[1], where[2], where[3])]
    return 2 if moved == [1, 1, 2] else 1


def solution(mesh):
    return jax.shard_map(
        functools.partial(on_device, chips_inner(mesh)),
        mesh=mesh,
        in_specs=(
            P("groups", "lat"),
            P("groups", "lat"),
            P(("groups", "lat")),
            P(("groups", "lat")),
            P(("groups", "lat"), None),
            P(("groups", "lat")),
            P("groups"),
        ),
        out_specs=(
            P("groups", "lat"),
            P(("groups", "lat")),
            P(("groups", "lat"), None),
            P(("groups", "lat")),
            P("groups"),
        ),
        check_vma=False,
    )
```

time: 282 us -> 133 us (0.47)
  waiting for transfers between devices: 188 us -> 0 us
  Pallas kernels: 0 us -> 121 us
  matrix products: 36.7 us -> 0 us
  blocking collectives: 30.6 us -> 0 us
  between operations: 15.7 us -> 2.61 us
    pallas_call x0 -> x2, Pallas kernels: none -> 121 us  [the longest x1 109 us: on_device(): pl.pallas_call(functools.partial(step_kernel, n, inner, rows), out_shape=...]
    reduce_scatter x1 -> x0, waiting for transfers between devices: 109 us -> none  [on_device(): lax.psum_scatter(partial_value, 'lat', scatter_dimension=1, tiled=True)]
    all_gather x2 -> x0, waiting for transfers between devices: 78.5 us -> none  [the longest x1 57.9 us: on_device(): lax.all_gather(inputs, 'lat', axis=1, tiled=True)]
    dot_general x5 -> x0, matrix products: 36.7 us -> none  [the longest x1 8.59 us: on_device(): partial_value = jnp.dot(feats, w_dec, preferred_element_type=jnp.float32)]
    psum x1 -> x0, blocking collectives: 30.6 us -> none  [on_device(): sq_sum, count_all = lax.psum((jnp.sum(err * err), count), 'lat')]
    unnamed x7 -> x4, local copies, waits for them, and re-layouts: 7.23 us -> 0.01 us
    reshape x0 -> x4, local copies, waits for them, and re-layouts: none -> 6.22 us  [the longest x1 1.69 us: on_device(): x_blocks = jnp.transpose(inputs.reshape(2, half, blk), (0, 2, 1))]
  transfers between devices with their start and end apart: 3 -> 0, of which waited for: 3 -> 0; matrix products, arithmetic and copies ran while one was open for 0% -> 0% of each run, Pallas kernels for 0% -> 0%
where the time goes in v1:
time: 133 us
  Pallas kernels  121 us (91%)
  local copies, waits for them, and re-layouts  7.5 us (6%)
  between operations  2.61 us (2%)
  other arithmetic  2.04 us (2%)
    pallas_call x1, Pallas kernels, on_device(): pl.pallas_call(functools.partial(step_kernel, n, inner, rows), out_shape=...  109 us
    pallas_call x1, Pallas kernels, on_device(): pl.pallas_call(grads_kernel, grid=(depth // tile,), out_shape=(jax.ShapeD...  11.9 us

profile of v1, /device:TPU:1, one launch (start us, length us, event | category | flops | bytes accessed | tf_op | source)
XLA Modules:
  0.0 132.9 jit_solution(5349867755651288646)
XLA Ops:
  0.6 1.7 %copy.18 = bf16[36,2,8,256]{3,2,0,1:T(8,128)(2,1)} copy(bf16[36,2,8,256]{3,2,1,0:T(8,128)(2,1)} %bitcast.15) | data formatting | bytes 589824 | tf_op jit(solution)/shard_map/reshape | solution.py:291
  2.3 1.5 %copy.13.benc_ref = f32[512,1]{1,0:T(8,128)} copy(f32[512,1]{0,1:T(1,128)} %bitcast.16) | data formatting | bytes 4096 | tf_op jit(solution)/shard_map/reshape | solution.py:333
  3.9 1.5 %copy.14.thr_ref = f32[512,1]{1,0:T(8,128)} copy(f32[512,1]{0,1:T(1,128)} %bitcast.17) | data formatting | bytes 4096 | tf_op jit(solution)/shard_map/reshape | solution.py:333
  5.4 1.4 %reshape.42.bdec_ref = f32[288,1]{1,0:T(8,128)} reshape(bf16[288]{0:T(512)(128)(2,1)} %param.12) | data formatting | bytes 1728 | tf_op jit(solution)/shard_map/reshape | solution.py:334
  6.9 108.9 %sae_step.1 = (bf16[2,4608,256]{2,1,0:T(8,128)(2,1)}, bf16[2,4608,256]{2,1,0:T(8,128)(2,1)}, bf16[2,512,256]{2,1,0:T(8,128)(2,1)}, bf16[2,512,256]{2,1,0:T(8,128...) custom-call(bf16[2,288,256]{2,1,0:T(8,128)(2,1)} %bitcast.14, bf16[4608,512]{1,0:T(8,128)(2,1)} %wenc_hbm.1, ...), custom_call_target="tpu_custom_call" | custom-call | tf_op jit(solution)/shard_map/sae_step/pallas_call | solution.py:295
  115.7 0.0 copy-start
  115.7 0.0 copy-start.1
  115.7 11.9 %sae_grads.1 = (bf16[4608,512]{1,0:T(8,128)(2,1)}, bf16[512,4608]{1,0:T(8,128)(2,1)}) custom-call(bf16[2,4608,256]{2,1,0:T(8,128)(2,1)} %get-tuple-element.14.xt_ref, bf16[2,4608,256]{2,1,0:T(8,128)(2,1)} %get-tuple-element.15.et_ref, bf16[2,512,256]{2,1,0:T(8,128)(2,1)} %get-tuple-element.16.ft_ref, bf16[2,512,256]{2,1,0:T(8,128)(2,1)} %get-tuple-element.17.gp_ref), custom_call_target="tpu_custom_call" | custom-call | tf_op jit(solution)/shard_map/sae_grads/pallas_call | solution.py:337
  127.6 1.3 fusion
  130.8 0.6 pad_maximum_fusion
  131.4 0.0 copy-done
  131.4 0.7 reduce
  132.2 0.0 copy-done.1
  132.2 0.7 reduce.1
Async XLA Ops:
  115.7 15.7 %copy-start = (f32[512,1]{1,0:T(8,128)S(1)}, f32[512,1]{1,0:T(8,128)}, u32[]{:S(2)}) copy-start(f32[512,1]{1,0:T(8,128)} %get-tuple-element.19) | copy-start | bytes 6148
  115.7 16.4 %copy-start.1 = (f32[288,1]{1,0:T(8,128)S(1)}, f32[288,1]{1,0:T(8,128)}, u32[]{:S(2)}) copy-start(f32[288,1]{1,0:T(8,128)} %get-tuple-element.21) | copy-start | bytes 3460

commit v2 on v1

--- a/solution.py
+++ b/solution.py
@@ -18,13 +18,13 @@
 
 def step_kernel(
     n, inner, rows_total,
-    x_ref, wenc_hbm, wdec_hbm, benc_ref, thr_ref, bdec_ref,
+    x_hbm, wenc_hbm, wdec_hbm, benc_ref, thr_ref, bdec_ref,
     xt_hbm, et_hbm, ft_ref, gp_ref, gbenc_ref, gbdec_ref, stats_ref,
     xt, et, wenc, wdec, wdt, pre, dg, theirs, given, mine, sbuf, rbuf, st,
     load_sem, out_sem,
     a_ss, a_rs, a_ds, a_dr, r_ss, r_rs, r_ds, r_dr, e_ss, e_rs, e_ds, e_dr,
 ):
-    blk, half = x_ref.shape[1], x_ref.shape[2]
+    blk, half = x_hbm.shape[0], x_hbm.shape[1] // 2
     depth, lat = wenc.shape
     subs = 2 if blk % 32 == 0 else 1
     sub_rows = blk // subs
@@ -59,11 +59,18 @@
     own_rows = pl.ds(pl.multiple_of(me * blk, 16), blk)
     load_enc = pltpu.make_async_copy(wenc_hbm, wenc, load_sem.at[0])
     load_dec = pltpu.make_async_copy(wdec_hbm, wdec, load_sem.at[1])
-    load_x = pltpu.make_async_copy(x_ref, xt.at[:, own_rows], load_sem.at[2])
-    load_x.start()
+    load_x = [
+        pltpu.make_async_copy(
+            x_hbm.at[:, pl.ds(h * half, half)], xt.at[h, own_rows], load_sem.at[2 + h]
+        )
+        for h in range(2)
+    ]
+    for h in range(2):
+        load_x[h].start()
     load_enc.start()
     load_dec.start()
-    load_x.wait()
+    for h in range(2):
+        load_x[h].wait()
     pl.semaphore_wait(barrier, 3)
 
     def remote(src, dst, ss, rs, peer):
@@ -73,7 +80,7 @@
         )
 
     def make_gather(buf, with_stats, ss, rs, ds, dr):
-        flows = [(h, u) for h in range(2) for u in range(subs)]
+        flows = [(h, u) for u in range(subs) for h in range(2)]
         if with_stats:
             flows.append((0, -1))
 
@@ -110,19 +117,25 @@
                 ring(f, 0).start()
             for f in count:
                 d2d(f, 0).start()
-            first()
 
             def arrive(s):
                 for f in count:
                     d2d_in(f, s).wait_recv()
 
-            @pl.loop(1, n - 1)
-            def _(s):
+            def forward(s):
                 for f in count:
                     ring_in(f, s - 1).wait_recv()
                     ring(f, s).start()
                     d2d(f, s).start()
                 arrive(s - 1)
+
+            forward(1)
+            first()
+            compute(0)
+
+            @pl.loop(2, n - 1)
+            def _(s):
+                forward(s)
                 compute(s - 1)
 
             for f in count:
@@ -147,16 +160,18 @@
 
     def first():
         pre[...] = jnp.zeros_like(pre)
+        load_enc.wait()
         load_dec.wait()
 
-        @pl.loop(0, depth // 128)
+    slices = depth // 128
+    each = pl.cdiv(slices, n)
+
+    def encode(s):
+        @pl.loop(s * each, jnp.minimum((s + 1) * each, slices))
         def _(i):
             c = pl.ds(pl.multiple_of(i * 128, 128), 128)
             wdt[c, :] = wdec[:, c].T
 
-        load_enc.wait()
-
-    def encode(s):
         for h in range(2):
             q = chip_at(pos - s if h == 0 else pos + s)
             r = pl.ds(pl.multiple_of(q * 2 * blk, 16), 2 * blk)
@@ -166,10 +181,13 @@
     out_x = pltpu.make_async_copy(xt, xt_hbm, out_sem.at[0])
     out_x.start()
 
+    benc = jnp.broadcast_to(benc_ref[...], (128, lat)).T[:, :1]
+    thr = jnp.broadcast_to(thr_ref[...], (128, lat)).T[:, :1]
+    bdec = jnp.broadcast_to(bdec_ref[...].astype(F32), (128, blk)).T[:, :1]
     total = jnp.zeros((1, half), F32)
     for h in range(2):
-        p = pre[h] + benc_ref[...]
-        gate = jax.nn.sigmoid((p - thr_ref[...]) / 0.05)
+        p = pre[h] + benc
+        gate = jax.nn.sigmoid((p - thr) / 0.05)
         ft_ref[h] = (p * gate).astype(BF16)
         dg[h] = gate + p * gate * (1.0 - gate) / 0.05
         total = total + jnp.sum(gate, axis=0, keepdims=True)
@@ -228,20 +246,26 @@
         swap(h, n - 1).wait_recv()
         for u in range(subs):
             pass_on(h, u, n - 2).wait_recv()
-        recon = mine[h, n - 1] + given[h, n - 1].astype(F32) + rbuf[h, n - 2].astype(F32) + bdec_ref[...]
-        err = recon - x_ref[h].astype(F32)
+        recon = mine[h, n - 1] + given[h, n - 1].astype(F32) + rbuf[h, n - 2].astype(F32) + bdec
+        err = recon - xt[h, own_rows, :].astype(F32)
         scaled = (2.0 / rows_total) * err
         et[h, own_rows, :] = scaled.astype(BF16)
         sq = sq + jnp.sum(err * err, axis=0, keepdims=True)
         gb = gb + jnp.sum(scaled, axis=1, keepdims=True)
-    gbdec_ref[...] = gb
+    gbdec_ref[...] = jnp.broadcast_to(gb, (blk, 128)).T[:1]
     lane = lax.broadcasted_iota(jnp.int32, (8, 128), 0)
     st[me] = jnp.where(lane == 0, jnp.sum(sq), jnp.sum(total))
 
-    def nothing(*_):
-        pass
-
-    make_gather(et, True, e_ss, e_rs, e_ds, e_dr)(nothing, nothing)
+    def clear():
+        pre[...] = jnp.zeros_like(pre)
+
+    def decode_back(s):
+        for h in range(2):
+            q = chip_at(pos - s if h == 0 else pos + s)
+            r = pl.ds(pl.multiple_of(q * 2 * blk, 16), 2 * blk)
+            pre[h] += dot(wdt[r, :], et[h, r, :], 0, 0)
+
+    make_gather(et, True, e_ss, e_rs, e_ds, e_dr)(clear, decode_back)
     out_e = pltpu.make_async_copy(et, et_hbm, out_sem.at[1])
     out_e.start()
 
@@ -256,28 +280,35 @@
         for h in range(2):
             swap(h, s).wait_send()
 
-    chunk = next(c for c in range(1152, 0, -128) if depth % c == 0)
     gsum = jnp.zeros((lat, 1), F32)
     for h in range(2):
-        pre[h] = jnp.zeros_like(pre[h])
-
-        @pl.loop(0, depth // chunk)
-        def _(i):
-            c = pl.ds(pl.multiple_of(i * chunk, 128), chunk)
-            pre[h] += dot(wdec[:, c], et[h, c, :], 1, 0)
-
         g = pre[h] * dg[h]
         gp_ref[h] = g.astype(BF16)
         gsum = gsum + jnp.sum(g, axis=1, keepdims=True)
-    gbenc_ref[...] = gsum
+    gbenc_ref[...] = jnp.broadcast_to(gsum, (lat, 128)).T[:1]
     stats_ref[...] = jnp.sum(st[...], axis=0)
     out_x.wait()
     out_e.wait()
 
 
-def grads_kernel(xt_ref, et_ref, ft_ref, gp_ref, genc_ref, gdec_ref):
+def grads_kernel(
+    sq_scale, gate_scale,
+    xt_ref, et_ref, ft_ref, gp_ref, gbenc_in, gbdec_in, stats_ref, spars_ref,
+    genc_ref, gdec_ref, gbenc_ref, gbdec_ref, loss_ref,
+):
     genc_ref[...] = (dot(xt_ref[0], gp_ref[0], 1, 1) + dot(xt_ref[1], gp_ref[1], 1, 1)).astype(BF16)
     gdec_ref[...] = (dot(ft_ref[0], et_ref[0], 1, 1) + dot(ft_ref[1], et_ref[1], 1, 1)).astype(BF16)
+
+    @pl.when(pl.program_id(0) == 0)
+    def _():
+        gbenc_ref[...] = gbenc_in[...]
+        gbdec_ref[...] = gbdec_in[...]
+        at = lax.broadcasted_iota(jnp.int32, (8, 128), 0)
+        lane = lax.broadcasted_iota(jnp.int32, (8, 128), 1)
+        v = stats_ref[...]
+        loss_ref[0] = jnp.sum(jnp.where((at == 0) & (lane == 0), v, 0.0)) * sq_scale
+        count = jnp.sum(jnp.where((at == 1) & (lane == 0), v, 0.0))
+        loss_ref[1] = spars_ref[0] * count * gate_scale
 
 
 def on_device(inner, inputs, w_enc, b_enc, thresholds, w_dec, b_dec, sparsity):
@@ -288,7 +319,6 @@
     half = rows // 2
     subs = 2 if blk % 32 == 0 else 1
     nf = 2 * subs
-    x_blocks = jnp.transpose(inputs.reshape(2, half, blk), (0, 2, 1))
     vmem = pl.BlockSpec(memory_space=pltpu.VMEM)
     hbm = pl.BlockSpec(memory_space=pl.ANY)
     dma = pltpu.SemaphoreType.DMA
@@ -299,11 +329,11 @@
             jax.ShapeDtypeStruct((2, depth, half), BF16),
             jax.ShapeDtypeStruct((2, lat, half), BF16),
             jax.ShapeDtypeStruct((2, lat, half), BF16),
-            jax.ShapeDtypeStruct((lat, 1), F32),
-            jax.ShapeDtypeStruct((blk, 1), F32),
+            jax.ShapeDtypeStruct((1, lat), F32),
+            jax.ShapeDtypeStruct((1, blk), F32),
             jax.ShapeDtypeStruct((8, 128), F32),
         ),
-        in_specs=[vmem, hbm, hbm, vmem, vmem, vmem],
+        in_specs=[hbm, hbm, hbm, vmem, vmem, vmem],
         out_specs=(hbm, hbm, vmem, vmem, vmem, vmem, vmem),
         scratch_shapes=[
             pltpu.VMEM((2, depth, half), BF16),
@@ -319,7 +349,7 @@
             pltpu.VMEM((2, n - 1, blk, half), BF16),
             pltpu.VMEM((2, n - 1, blk, half), BF16),
             pltpu.VMEM((parts, 8, 128), F32),
-            dma((3,)),
+            dma((4,)),
             dma((2,)),
             dma((nf, n - 1)), dma((nf, n - 1)), dma((nf, n)), dma((nf, n)),
             dma((nf, n - 1)), dma((nf, n - 1)), dma((2, n)), dma((2, n)),
@@ -330,36 +360,42 @@
         ),
         name="sae_step",
     )(
-        x_blocks, w_enc, w_dec, b_enc.reshape(lat, 1), thresholds.reshape(lat, 1),
-        b_dec.astype(F32).reshape(blk, 1),
+        inputs.T, w_enc, w_dec, b_enc.reshape(1, lat), thresholds.reshape(1, lat),
+        b_dec.reshape(1, blk),
     )
     tile = 512 if depth % 512 == 0 else 128
-    grad_enc, grad_dec = pl.pallas_call(
-        grads_kernel,
+    row = lambda width: pl.BlockSpec((1, width), lambda i: (0, 0))
+    smem = pl.BlockSpec(memory_space=pltpu.SMEM)
+    grad_enc, grad_dec, grad_b_enc, grad_b_dec, loss_terms = pl.pallas_call(
+        functools.partial(grads_kernel, 1.0 / (rows * depth), 1.0 / (rows * lat * parts)),
         grid=(depth // tile,),
         out_shape=(
             jax.ShapeDtypeStruct((depth, lat), BF16),
             jax.ShapeDtypeStruct((lat, depth), BF16),
+            jax.ShapeDtypeStruct((1, lat), F32),
+            jax.ShapeDtypeStruct((1, blk), F32),
+            jax.ShapeDtypeStruct((2,), F32),
         ),
         in_specs=[
             pl.BlockSpec((2, tile, half), lambda i: (0, i, 0)),
             pl.BlockSpec((2, tile, half), lambda i: (0, i, 0)),
             pl.BlockSpec((2, lat, half), lambda i: (0, 0, 0)),
             pl.BlockSpec((2, lat, half), lambda i: (0, 0, 0)),
+            row(lat),
+            row(blk),
+            pl.BlockSpec((8, 128), lambda i: (0, 0)),
+            smem,
         ],
         out_specs=(
             pl.BlockSpec((tile, lat), lambda i: (i, 0)),
             pl.BlockSpec((lat, tile), lambda i: (0, i)),
+            row(lat),
+            row(blk),
+            smem,
         ),
         name="sae_grads",
-    )(xt, et, ft, gp)
-    loss_terms = jnp.stack(
-        [
-            stats[0, 0] / (rows * depth),
-            sparsity[0] * stats[1, 0] / (rows * lat * parts),
-        ]
-    )
-    return grad_enc, gbenc.reshape(lat), grad_dec, gbdec.reshape(blk), loss_terms
+    )(xt, et, ft, gp, gbenc, gbdec, stats, sparsity)
+    return grad_enc, grad_b_enc.reshape(lat), grad_dec, grad_b_dec.reshape(blk), loss_terms
 
 
 def chips_inner(mesh):

time: 133 us -> 117 us (0.88)
  Pallas kernels: 121 us -> 113 us
  local copies, waits for them, and re-layouts: 7.5 us -> 1.24 us
    pallas_call x1, Pallas kernels: 109 us -> 100 us  [on_device(): pl.pallas_call(functools.partial(step_kernel, n, inner, rows), out_shape=...]
    reshape x4 -> x1, local copies, waits for them, and re-layouts: 6.22 us -> 1.24 us  [on_device(): b_dec.reshape(1, blk)]
where the time goes in v2:
time: 117 us
  Pallas kernels  113 us (97%)
  between operations  1.29 us (1%)
  other arithmetic  1.27 us (1%)
  local copies, waits for them, and re-layouts  1.24 us (1%)
    pallas_call x1, Pallas kernels, on_device(): pl.pallas_call(functools.partial(step_kernel, n, inner, rows), out_shape=...  100 us
    pallas_call x1, Pallas kernels, on_device(): pl.pallas_call(functools.partial(grads_kernel, 1.0 / (rows * depth), 1.0...  12.9 us

profile of v2, /device:TPU:1, one launch (start us, length us, event | category | flops | bytes accessed | tf_op | source)
XLA Modules:
  0.0 116.9 jit_solution(3720698050274377814)
XLA Ops:
  1.3 1.2 %reshape.27.bdec_ref = bf16[1,288]{1,0:T(2,128)(2,1)} reshape(bf16[288]{0:T(512)(128)(2,1)} %param.12) | data formatting | bytes 1152 | tf_op jit(solution)/shard_map/reshape | solution.py:364
  2.5 100.2 %sae_step.1 = (bf16[2,4608,256]{2,1,0:T(8,128)(2,1)}, bf16[2,4608,256]{2,1,0:T(8,128)(2,1)}, bf16[2,512,256]{2,1,0:T(8,128)(2,1)}, bf16[2,512,256]{2,1,0:T(8,128...) custom-call(bf16[288,512]{1,0:T(8,128)(2,1)} %bitcast.4, bf16[4608,512]{1,0:T(8,128)(2,1)} %wenc_hbm.1, ...), custom_call_target="tpu_custom_call" | custom-call | tf_op jit(solution)/shard_map/sae_step/pallas_call | solution.py:325
  102.7 12.9 %sae_grads.1 = (bf16[4608,512]{1,0:T(8,128)(2,1)}, bf16[512,4608]{1,0:T(8,128)(2,1)}, f32[1,512]{1,0:T(1,128)}, f32[1,288]{1,0:T(1,128)}, f32[2]{0:T(128)}) custom-call(bf16[2,4608,256]{2,1,0:T(8,128)(2,1)} %get-tuple-element.17.xt_ref, bf16[2,4608,256]{2,1,0:T(8,128)(2,1)} %get-tuple-element.18.et_ref, bf16[2,512,256]{2,1,0:T(8,128)(2,1)} %get-tuple-element.19.ft_ref, ...), custom_call_target="tpu_custom_call" | custom-call | tf_op jit(solution)/shard_map/sae_grads/pallas_call | solution.py:369
  115.6 1.3 %reduce = f32[288]{0:T(512)} reduce(f32[1,288]{1,0:T(1,128)} %get-tuple-element.27, f32[]{:T(128)} %constant.1), dimensions={0}, to_apply=%get-tuple-element.27.reduce_sub_computation | reduce | bytes 2308 | tf_op jit(solution)/shard_map/sae_grads/pallas_call | solution.py:369

commit v3 on v2

--- a/solution.py
+++ b/solution.py
@@ -19,9 +19,9 @@
 def step_kernel(
     n, inner, rows_total,
     x_hbm, wenc_hbm, wdec_hbm, benc_ref, thr_ref, bdec_ref,
-    xt_hbm, et_hbm, ft_ref, gp_ref, gbenc_ref, gbdec_ref, stats_ref,
-    xt, et, wenc, wdec, wdt, pre, dg, theirs, given, mine, sbuf, rbuf, st,
-    load_sem, out_sem,
+    xt, et, ft_ref, gp_ref, gbenc_ref, gbdec_ref, stats_ref,
+    wenc, wdec, wdt, pre, dg, theirs, given, mine, sbuf, rbuf, st,
+    load_sem,
     a_ss, a_rs, a_ds, a_dr, r_ss, r_rs, r_ds, r_dr, e_ss, e_rs, e_ds, e_dr,
 ):
     blk, half = x_hbm.shape[0], x_hbm.shape[1] // 2
@@ -178,8 +178,6 @@
             pre[h] += dot(wenc[r, :], xt[h, r, :], 0, 0)
 
     make_gather(xt, False, a_ss, a_rs, a_ds, a_dr)(first, encode)
-    out_x = pltpu.make_async_copy(xt, xt_hbm, out_sem.at[0])
-    out_x.start()
 
     benc = jnp.broadcast_to(benc_ref[...], (128, lat)).T[:, :1]
     thr = jnp.broadcast_to(thr_ref[...], (128, lat)).T[:, :1]
@@ -266,8 +264,6 @@
             pre[h] += dot(wdt[r, :], et[h, r, :], 0, 0)
 
     make_gather(et, True, e_ss, e_rs, e_ds, e_dr)(clear, decode_back)
-    out_e = pltpu.make_async_copy(et, et_hbm, out_sem.at[1])
-    out_e.start()
 
     @pl.loop(0, n - 1)
     def _(s):
@@ -287,8 +283,6 @@
         gsum = gsum + jnp.sum(g, axis=1, keepdims=True)
     gbenc_ref[...] = jnp.broadcast_to(gsum, (lat, 128)).T[:1]
     stats_ref[...] = jnp.sum(st[...], axis=0)
-    out_x.wait()
-    out_e.wait()
 
 
 def grads_kernel(
@@ -296,8 +290,14 @@
     xt_ref, et_ref, ft_ref, gp_ref, gbenc_in, gbdec_in, stats_ref, spars_ref,
     genc_ref, gdec_ref, gbenc_ref, gbdec_ref, loss_ref,
 ):
-    genc_ref[...] = (dot(xt_ref[0], gp_ref[0], 1, 1) + dot(xt_ref[1], gp_ref[1], 1, 1)).astype(BF16)
-    gdec_ref[...] = (dot(ft_ref[0], et_ref[0], 1, 1) + dot(ft_ref[1], et_ref[1], 1, 1)).astype(BF16)
+    tile = genc_ref.shape[0]
+    r = pl.ds(pl.multiple_of(pl.program_id(0) * tile, 16), tile)
+    genc_ref[...] = (
+        dot(xt_ref[0, r, :], gp_ref[0], 1, 1) + dot(xt_ref[1, r, :], gp_ref[1], 1, 1)
+    ).astype(BF16)
+    gdec_ref[...] = (
+        dot(ft_ref[0], et_ref[0, r, :], 1, 1) + dot(ft_ref[1], et_ref[1, r, :], 1, 1)
+    ).astype(BF16)
 
     @pl.when(pl.program_id(0) == 0)
     def _():
@@ -325,19 +325,17 @@
     xt, et, ft, gp, gbenc, gbdec, stats = pl.pallas_call(
         functools.partial(step_kernel, n, inner, rows),
         out_shape=(
-            jax.ShapeDtypeStruct((2, depth, half), BF16),
-            jax.ShapeDtypeStruct((2, depth, half), BF16),
-            jax.ShapeDtypeStruct((2, lat, half), BF16),
-            jax.ShapeDtypeStruct((2, lat, half), BF16),
+            pltpu.VMEM((2, depth, half), BF16),
+            pltpu.VMEM((2, depth, half), BF16),
+            pltpu.VMEM((2, lat, half), BF16),
+            pltpu.VMEM((2, lat, half), BF16),
             jax.ShapeDtypeStruct((1, lat), F32),
             jax.ShapeDtypeStruct((1, blk), F32),
             jax.ShapeDtypeStruct((8, 128), F32),
         ),
         in_specs=[hbm, hbm, hbm, vmem, vmem, vmem],
-        out_specs=(hbm, hbm, vmem, vmem, vmem, vmem, vmem),
+        out_specs=(vmem, vmem, vmem, vmem, vmem, vmem, vmem),
         scratch_shapes=[
-            pltpu.VMEM((2, depth, half), BF16),
-            pltpu.VMEM((2, depth, half), BF16),
             pltpu.VMEM((depth, lat), BF16),
             pltpu.VMEM((lat, depth), BF16),
             pltpu.VMEM((depth, lat), BF16),
@@ -350,13 +348,12 @@
             pltpu.VMEM((2, n - 1, blk, half), BF16),
             pltpu.VMEM((parts, 8, 128), F32),
             dma((4,)),
-            dma((2,)),
             dma((nf, n - 1)), dma((nf, n - 1)), dma((nf, n)), dma((nf, n)),
             dma((nf, n - 1)), dma((nf, n - 1)), dma((2, n)), dma((2, n)),
             dma((nf + 1, n - 1)), dma((nf + 1, n - 1)), dma((nf + 1, n)), dma((nf + 1, n)),
         ],
         compiler_params=pltpu.CompilerParams(
-            collective_id=0, has_side_effects=True, vmem_limit_bytes=63 * 1024 * 1024
+            collective_id=0, has_side_effects=True, vmem_limit_bytes=44 * 1024 * 1024
         ),
         name="sae_step",
     )(
@@ -377,10 +374,10 @@
             jax.ShapeDtypeStruct((2,), F32),
         ),
         in_specs=[
-            pl.BlockSpec((2, tile, half), lambda i: (0, i, 0)),
-            pl.BlockSpec((2, tile, half), lambda i: (0, i, 0)),
-            pl.BlockSpec((2, lat, half), lambda i: (0, 0, 0)),
-            pl.BlockSpec((2, lat, half), lambda i: (0, 0, 0)),
+            vmem,
+            vmem,
+            vmem,
+            vmem,
             row(lat),
             row(blk),
             pl.BlockSpec((8, 128), lambda i: (0, 0)),
@@ -393,6 +390,7 @@
             row(blk),
             smem,
         ),
+        compiler_params=pltpu.CompilerParams(vmem_limit_bytes=16 * 1024 * 1024),
         name="sae_grads",
     )(xt, et, ft, gp, gbenc, gbdec, stats, sparsity)
     return grad_enc, grad_b_enc.reshape(lat), grad_dec, grad_b_dec.reshape(blk), loss_terms

time: 117 us -> 112 us (0.957)
  Pallas kernels: 113 us -> 107 us
  local copies, waits for them, and re-layouts: 1.24 us -> 3.24 us
    pallas_call x1, Pallas kernels: 12.9 us -> 8.59 us  [on_device(): pl.pallas_call(functools.partial(grads_kernel, 1.0 / (rows * depth), 1.0...]
    pallas_call x1, Pallas kernels: 100 us -> 98 us  [on_device(): pl.pallas_call(functools.partial(step_kernel, n, inner, rows), out_shape=...]
    unnamed x0 -> x6, local copies, waits for them, and re-layouts: none -> 1.99 us
where the time goes in v3:
time: 112 us
  Pallas kernels  107 us (96%)
  local copies, waits for them, and re-layouts  3.24 us (3%)
  between operations  1.3 us (1%)
    pallas_call x1, Pallas kernels, on_device(): pl.pallas_call(functools.partial(step_kernel, n, inner, rows), out_shape=...  98 us
    pallas_call x1, Pallas kernels, on_device(): pl.pallas_call(functools.partial(grads_kernel, 1.0 / (rows * depth), 1.0...  8.59 us

profile of v3, /device:TPU:1, one launch (start us, length us, event | category | flops | bytes accessed | tf_op | source)
XLA Modules:
  0.0 111.7 jit_solution(13268190747363269637)
XLA Ops:
  1.3 1.2 %reshape.27.bdec_ref = bf16[1,288]{1,0:T(2,128)(2,1)} reshape(bf16[288]{0:T(512)(128)(2,1)} %param.12) | data formatting | bytes 1152 | tf_op jit(solution)/shard_map/reshape | solution.py:361
  2.5 98.0 %sae_step.1 = (bf16[2,4608,256]{2,1,0:T(8,128)(2,1)S(1)}, bf16[2,4608,256]{2,1,0:T(8,128)(2,1)S(1)}, bf16[2,512,256]{2,1,0:T(8,128)(2,1)S(1)}, bf16[2,512,256]{2...) custom-call(bf16[288,512]{1,0:T(8,128)(2,1)} %bitcast.4, ...), custom_call_target="tpu_custom_call" | custom-call | tf_op jit(solution)/shard_map/sae_step/pallas_call | solution.py:325
  100.5 0.0 copy-start
  100.6 0.7 copy-done
  101.2 0.0 copy-start.1
  101.2 0.7 copy-done.1
  101.9 0.0 copy-start.2
  101.9 0.7 copy-done.2
  102.5 8.6 %sae_grads.1 = (bf16[4608,512]{1,0:T(8,128)(2,1)}, bf16[512,4608]{1,0:T(8,128)(2,1)}, f32[1,512]{1,0:T(1,128)}, f32[1,288]{1,0:T(1,128)S(1)}, f32[2]{0:T(128)}) custom-call(bf16[2,4608,256]{2,1,0:T(8,128)(2,1)S(1)} %get-tuple-element.17.xt_ref, bf16[2,4608,256]{2,1,0:T(8,128)(2,1)S(1)} %get-tuple-element.18.et_ref, ...), custom_call_target="tpu_custom_call" | custom-call | tf_op jit(solution)/shard_map/sae_grads/pallas_call | solution.py:366
  111.1 0.6 reduce
Async XLA Ops:
  100.5 0.7 copy-start
  101.2 0.7 copy-start.1
  101.9 0.7 copy-start.2
